TPU v7x, 512 devices: a whole 4x8x8 slice. The times are simulated.
512 devices in a mesh: sub: 8 (over y), row: 8 (over x, core), col: 8 (over z).
Axes of the slice: x: 4, y: 8, z: 8, core: 2. Of those that a mesh axis runs over, the one named last changes fastest.
Arguments:
- visibility: bfloat16 [2, 64, 512, 4096], P(None, 'sub', 'row', 'col'), may hold values from -13 to 13
- sky_model: bfloat16 [2, 64, 512, 4096], P(None, 'sub', 'row', 'col'), may hold values from -4 to 4, as said below
- antenna_flags: int32 [8, 512], P('sub'), may hold values 0 or 1
- gains_init: float32 [2, 64, 512], P(None, 'sub'), may hold values from -0.5 to 1.5
Outputs:
- gains: float32 [2, 64, 512], P(None, 'sub')
Inputs may be any that keep to these rules, and one draw needn't show every extreme that they name: `sky_model`: model visibility parts lie between -4 and 4.
All inputs are finite; a program needn't handle non-finite values.
Results may differ from a plain program's by a relative error of at most 0.0003.
Values sent between devices are 32-bit elements.
A program may use at most 64 MiB of HBM per device.

v0:
```python
import jax
import jax.numpy as jnp
from jax import lax
from jax.sharding import PartitionSpec as P

TIMES = 8
ITERS = 3


def copy_for_each(array, axis):
    devices = lax.axis_size(axis)
    return lax.all_to_all(
        jnp.broadcast_to(array[None], (devices, *array.shape)), axis, 0, 0, tiled=True
    )


def of_everyone(array, axis):
    return copy_for_each(array, axis).sum(axis=0)


def in_order(blocks, dim):
    shape = list(blocks.shape[1:])
    shape[dim] *= blocks.shape[0]
    return jnp.moveaxis(blocks, 0, dim).reshape(shape)


def collect(array, axis, dim):
    return in_order(copy_for_each(array, axis), dim)


def subband_total(values):
    return of_everyone(values, "sub")


def update_gains(summed, previous):
    denominator = summed[:, 2, :] + 1.0
    quotient = jnp.stack([summed[:, 0, :] / denominator, summed[:, 1, :] / denominator], axis=0)
    updated = 0.5 * (quotient + previous)
    chan_mean = jnp.sum(updated, axis=1) / updated.shape[1]
    overall = subband_total(chan_mean) / lax.axis_size("sub")
    return updated + 0.5 * (overall - chan_mean)[:, None, :]


def time_total(values, selector):
    return jnp.einsum(
        "crk,kq->crq",
        values,
        selector,
        precision=lax.Precision.HIGHEST,
        preferred_element_type=jnp.float32,
    )


def contract(matrix, vector):
    return jnp.einsum("cpq,cq->cp", matrix, vector, precision=lax.Precision.HIGHEST)


def body(visibility, sky_model, antenna_flags, gains_init):
    block_rows = visibility.shape[2]
    wide_cols = visibility.shape[3]
    block_cols = wide_cols // TIMES
    row_at = lax.axis_index("row") * block_rows
    col_at = lax.axis_index("col") * block_cols
    flag_value = antenna_flags[0].astype(jnp.float32)
    row_flag = lax.dynamic_slice_in_dim(flag_value, row_at, block_rows)
    col_flag = lax.dynamic_slice_in_dim(flag_value, col_at, block_cols)
    row_ids = row_at + lax.iota(jnp.int32, block_rows)
    col_ids = col_at + lax.iota(jnp.int32, block_cols)
    weight = (
        row_flag[:, None]
        * col_flag[None, :]
        * (row_ids[:, None] != col_ids[None, :]).astype(jnp.float32)
    )
    selector = (
        lax.iota(jnp.int32, wide_cols)[:, None] // TIMES == lax.iota(jnp.int32, block_cols)[None, :]
    ).astype(jnp.float32)
    vis_re = visibility[0].astype(jnp.float32)
    vis_im = visibility[1].astype(jnp.float32)
    mod_re = sky_model[0].astype(jnp.float32)
    mod_im = sky_model[1].astype(jnp.float32)
    cross_re = time_total(vis_re * mod_re + vis_im * mod_im, selector) * weight
    cross_im = time_total(vis_im * mod_re - vis_re * mod_im, selector) * weight
    power_sum = time_total(mod_re * mod_re + mod_im * mod_im, selector) * weight
    gain_values = gains_init
    for step_index in range(ITERS):
        col_gains = lax.dynamic_slice_in_dim(gain_values, col_at, block_cols, 2)
        gain_re = col_gains[0]
        gain_im = col_gains[1]
        num_re = contract(cross_re, gain_re) - contract(cross_im, gain_im)
        num_im = contract(cross_re, gain_im) + contract(cross_im, gain_re)
        denominator = contract(power_sum, gain_re * gain_re + gain_im * gain_im)
        partial_value = jnp.stack([num_re, num_im, denominator], axis=1)
        summed = of_everyone(partial_value, "col")
        previous = lax.dynamic_slice_in_dim(gain_values, row_at, block_rows, 2)
        gain_block = update_gains(summed, previous)
        gain_values = collect(gain_block, "row", 2)
    return gain_values


def solution(mesh):
    return jax.shard_map(
        body,
        mesh=mesh,
        in_specs=(
            P(None, "sub", "row", "col"),
            P(None, "sub", "row", "col"),
            P("sub", None),
            P(None, "sub", None),
        ),
        out_specs=P(None, "sub", None),
        check_vma=False,
    )
```

profile of v0, /device:TPU:1, one launch (start us, length us, event | category | flops | bytes accessed | tf_op | source)
XLA Modules:
  0.0 123.8 jit_solution(15700047814634009049)
XLA Ops:
  0.0 0.7 copy-done.1
  0.8 0.1 multiply_select_fusion
  0.9 2.5 %convolution_multiply_fusion.1 = f32[8,64,64]{2,1,0:T(8,128)S(1)} fusion(bf16[2,8,64,512]{3,2,1,0:T(8,128)(2,1)} %param.4, bf16[2,8,64,512]{3,2,1,0:T(8,128)(2,1)} %param.5, f32[64,64]{1,0:T(8,128)S(1)} %multiply_select_fusion, s32[512]{0:T(512)S(1)} %add_select_fusion), kind=kOutput, calls=%fused_computation.7 | convolution fusion | flops 203227136 | bytes 2246656 | tf_op jit(solution)/shard_map/crk,kq->crq/dot_general | solution.py:45
  3.4 0.8 convolution_multiply_fusion.2
  4.2 0.1 fusion.37
  4.3 0.5 fusion.49
  4.8 0.5 fusion.47
  5.4 0.5 fusion.48
  5.9 0.5 fusion.46
  6.4 0.8 convolution_multiply_fusion
  7.2 0.5 fusion.50
  7.8 0.1 reshape.309
  7.9 17.7 %all_to_all.45 = f32[8,1,1536]{2,1,0:T(1,128)S(1)} all-to-all(f32[8,1,1536]{2,1,0:T(1,128)S(1)} %reshape.309), channel_id=1, replica_groups=mesh['sub'=8,'row'=8,'col'=8] {'col'}, dimensions={0} | all-to-all | bytes 98304 | tf_op jit(solution)/shard_map/all_to_all | solution.py:12
  25.6 0.5 broadcast.242
  26.1 0.8 reduce
  26.9 0.1 reshape.310
  27.0 0.1 fusion.43
  27.1 0.1 reshape.311
  27.2 13.2 %all_to_all.46 = f32[8,1,128]{2,1,0:T(1,128)S(1)} all-to-all(f32[8,1,128]{2,1,0:T(1,128)S(1)} %reshape.311), channel_id=1, replica_groups=mesh['sub'=8,'row'=8,'col'=8] {'sub'}, dimensions={0} | all-to-all | bytes 8192 | tf_op jit(solution)/shard_map/all_to_all | solution.py:12
  40.3 0.7 reduce.1
  41.0 0.1 reshape.312
  41.1 0.1 broadcast_add_fusion.2
  41.2 0.1 reshape.313
  41.3 12.3 %all_to_all.47 = f32[8,1,1024]{2,1,0:T(1,128)S(1)} all-to-all(f32[8,1,1024]{2,1,0:T(1,128)S(1)} %reshape.313), channel_id=1, replica_groups=mesh['sub'=8,'row'=8,'col'=8] {'row'}, dimensions={0} | all-to-all | bytes 65536 | tf_op jit(solution)/shard_map/all_to_all | solution.py:12
  53.7 0.7 reduce.2
  54.5 0.1 reshape.281
  54.7 0.5 fusion.54
  55.2 0.5 fusion.51
  55.7 0.5 fusion.53
  56.2 0.5 fusion.52
  56.8 0.5 fusion.55
  57.3 0.1 reshape.315
  57.4 9.5 %all_to_all.48 = f32[8,1,1536]{2,1,0:T(1,128)S(1)} all-to-all(f32[8,1,1536]{2,1,0:T(1,128)S(1)} %reshape.315), channel_id=1, replica_groups=mesh['sub'=8,'row'=8,'col'=8] {'col'}, dimensions={0} | all-to-all | bytes 98304 | tf_op jit(solution)/shard_map/all_to_all | solution.py:12
  66.9 0.8 reduce.3
  67.7 0.1 reshape.316
  67.8 0.1 fusion.42
  67.9 0.1 reshape.317
  68.0 8.9 %all_to_all.49 = f32[8,1,128]{2,1,0:T(1,128)S(1)} all-to-all(f32[8,1,128]{2,1,0:T(1,128)S(1)} %reshape.317), channel_id=1, replica_groups=mesh['sub'=8,'row'=8,'col'=8] {'sub'}, dimensions={0} | all-to-all | bytes 8192 | tf_op jit(solution)/shard_map/all_to_all | solution.py:12
  76.9 0.7 reduce.4
  77.6 0.1 reshape.318
  77.7 0.1 broadcast_add_fusion.1
  77.8 0.1 reshape.319
  77.9 10.1 %all_to_all.50 = f32[8,1,1024]{2,1,0:T(1,128)S(1)} all-to-all(f32[8,1,1024]{2,1,0:T(1,128)S(1)} %reshape.319), channel_id=1, replica_groups=mesh['sub'=8,'row'=8,'col'=8] {'row'}, dimensions={0} | all-to-all | bytes 65536 | tf_op jit(solution)/shard_map/all_to_all | solution.py:12
  88.0 0.7 reduce.5
  88.7 0.1 reshape.320
  88.9 0.5 fusion.57
  89.5 0.5 fusion.58
  90.0 0.5 fusion.59
  90.5 0.5 fusion.56
  91.0 0.5 fusion.60
  91.6 0.1 reshape.321
  91.7 9.5 %all_to_all.51 = f32[8,1,1536]{2,1,0:T(1,128)S(1)} all-to-all(f32[8,1,1536]{2,1,0:T(1,128)S(1)} %reshape.321), channel_id=1, replica_groups=mesh['sub'=8,'row'=8,'col'=8] {'col'}, dimensions={0} | all-to-all | bytes 98304 | tf_op jit(solution)/shard_map/all_to_all | solution.py:12
  101.2 0.8 reduce.6
  102.0 0.1 reshape.322
  102.1 0.1 fusion.41
  102.2 0.1 reshape.323
  102.3 8.9 %all_to_all.52 = f32[8,1,128]{2,1,0:T(1,128)S(1)} all-to-all(f32[8,1,128]{2,1,0:T(1,128)S(1)} %reshape.323), channel_id=1, replica_groups=mesh['sub'=8,'row'=8,'col'=8] {'sub'}, dimensions={0} | all-to-all | bytes 8192 | tf_op jit(solution)/shard_map/all_to_all | solution.py:12
  111.2 0.7 reduce.7
  111.9 0.1 reshape.324
  112.0 0.1 broadcast_add_fusion
  112.1 0.1 reshape.325
  112.2 10.1 %all_to_all.53 = f32[8,1,1024]{2,1,0:T(1,128)S(1)} all-to-all(f32[8,1,1024]{2,1,0:T(1,128)S(1)} %reshape.325), channel_id=1, replica_groups=mesh['sub'=8,'row'=8,'col'=8] {'row'}, dimensions={0} | all-to-all | bytes 65536 | tf_op jit(solution)/shard_map/all_to_all | solution.py:12
  122.2 0.7 reduce.8
  123.1 0.7 reshape.283
  (52 shorter events, 0.9 us)
Async XLA Ops:
  0.0 0.7 copy-start.1
  0.8 2.5 %copy-start.2 = (bf16[2,8,64,512]{3,2,1,0:T(8,128)(2,1)S(1)}, bf16[2,8,64,512]{3,2,1,0:T(8,128)(2,1)}, u32[]{:S(2)}) copy-start(bf16[2,8,64,512]{3,2,1,0:T(8,128)(2,1)} %param.4) | copy-start | bytes 3145732
  0.9 2.5 %copy-start.3 = (bf16[2,8,64,512]{3,2,1,0:T(8,128)(2,1)S(1)}, bf16[2,8,64,512]{3,2,1,0:T(8,128)(2,1)}, u32[]{:S(2)}) copy-start(bf16[2,8,64,512]{3,2,1,0:T(8,128)(2,1)} %param.5) | copy-start | bytes 3145732
  3.4 0.8 copy-start
where the time goes:
time: 124 us
  blocking collectives  100 us (81%)
  matrix products  11.9 us (10%)
  other arithmetic  7.49 us (6%)
  local copies, waits for them, and re-layouts  3.88 us (3%)
    all_to_all x9, blocking collectives, copy_for_each(): lax.all_to_all(jnp.broadcast_to(array[None], (devices, *array.shape)), ax...  100 us
    dot_general x15, matrix products, contract(): jnp.einsum('cpq,cq->cp', matrix, vector, precision=lax.Precision.HIGHEST)  7.86 us
    all_to_all x9, other arithmetic, copy_for_each(): lax.all_to_all(jnp.broadcast_to(array[None], (devices, *array.shape)), ax...  6.41 us
    dot_general x3, matrix products, time_total(): jnp.einsum('crk,kq->crq', values, selector, precision=lax.Precision.HIGHE...  4.08 us

commit v1 on v0

v1 whole, which is shorter than its diff:
```python
import functools

import jax
import jax.numpy as jnp
from jax import lax
from jax.experimental import pallas as pl
from jax.experimental.pallas import tpu as pltpu
from jax.sharding import PartitionSpec as P

TIMES = 8
ITERS = 3
MESH = pl.DeviceIdType.MESH


def far_first(n):
    return sorted(range(1, n), key=lambda d: (-min(d, n - d), d))


def kernel(
    sizes,
    vis_ref, sky_ref, flag_ref, init_ref, out_ref,
    vis, sky, prod, cross_re, cross_im, power, spread,
    zsend, zbuf, ysend, ybuf, gsend, gbuf, pbuf, fsend, fbuf,
    in_sem, z_ssem, z_rsem, y_ssem, y_rsem, g_ssem, g_rsem, p_ssem, p_rsem, f_ssem, f_rsem,
):
    n_sub, n_row, n_col, block, channels = sizes
    half = channels // 2
    f32, bf16 = jnp.float32, jnp.bfloat16
    sub, row, col = lax.axis_index("sub"), lax.axis_index("row"), lax.axis_index("col")
    hub = row == col
    wide = block * TIMES
    lanes = 2 * block

    loads = []
    for c in [j + half * h for j in range(half) for h in range(2)]:
        for a, (src, dst) in enumerate(((vis_ref, vis), (sky_ref, sky))):
            copy = pltpu.make_async_copy(src.at[:, c], dst.at[:, c], in_sem.at[a, c])
            copy.start()
            loads.append(((a, c), copy))
    loads = dict(loads)

    barrier = pltpu.get_barrier_semaphore()
    for axis, me, n in (("col", col, n_col), ("sub", sub, n_sub), ("row", row, n_row)):
        for d in far_first(n):
            pl.semaphore_signal(barrier, inc=1, device_id={axis: lax.rem(me + d, n)}, device_id_type=MESH)

    lane = lax.broadcasted_iota(jnp.int32, (1, lanes), 1)
    low = lane < block

    def pick(array, index, n):
        total = jnp.where(index == 0, array[..., 0:block], 0.0)
        for k in range(1, n):
            total = total + jnp.where(index == k, array[..., k * block : (k + 1) * block], 0.0)
        return total

    init = pick(init_ref[...], col, n_col)
    start_gains = jnp.concatenate(
        [jnp.concatenate([init[i, :half], init[i, half:]], axis=1) for i in range(2)], axis=0
    )

    flags = flag_ref[...].astype(f32)
    row_flag = pick(flags, row, n_row)
    row_flag = jnp.concatenate([row_flag, row_flag], axis=1)
    col_flag = pick(flags, col, n_col)
    diagonal = lax.broadcasted_iota(jnp.int32, (block, block), 0) == lax.broadcasted_iota(
        jnp.int32, (block, block), 1
    )
    col_flag = jnp.sum(jnp.where(diagonal, col_flag, 0.0), axis=1, keepdims=True)
    q_id = col * block + lax.broadcasted_iota(jnp.int32, (block, lanes), 0)
    p_id = row * block + lax.rem(lax.broadcasted_iota(jnp.int32, (block, lanes), 1), block)
    weight = jnp.where(q_id != p_id, col_flag * row_flag, 0.0)

    rows_k = 6 * channels
    k_id = lax.broadcasted_iota(jnp.int32, (rows_k, channels * lanes), 0)
    n_id = lax.broadcasted_iota(jnp.int32, (rows_k, channels * lanes), 1)
    spread[...] = jnp.where(
        (lax.rem(k_id, channels) == n_id // lanes)
        & (lax.rem(k_id // channels, 2) == lax.rem(n_id, lanes) // block),
        1.0,
        0.0,
    ).astype(bf16)

    def expand(gains):
        both = jnp.concatenate([gains[:, :block], gains[:, block:]], axis=0)
        high = both.astype(bf16)
        rest = both - high.astype(f32)
        mid = rest.astype(bf16)
        last = (rest - mid.astype(f32)).astype(bf16)
        pieces = jnp.concatenate([high, mid, last], axis=0)
        return lax.dot_general(
            pieces, spread[...], (((0,), (0,)), ((), ())), preferred_element_type=f32
        )

    def contract(step, wide_gains, j):
        g_re = wide_gains[:, j * lanes : (j + 1) * lanes]
        g_im = wide_gains[:, (half + j) * lanes : (half + j + 1) * lanes]
        c_re, c_im, c_pow = cross_re[j], cross_im[j], power[j]
        zsend[step, j : j + 1] = jnp.sum(c_re * g_re - c_im * g_im, axis=0, keepdims=True)
        zsend[step, half + j : half + j + 1] = jnp.sum(c_re * g_im + c_im * g_re, axis=0, keepdims=True)
        zsend[step, channels + j : channels + j + 1] = jnp.sum(
            c_pow * (g_re * g_re + g_im * g_im), axis=0, keepdims=True
        )

    kt = 2
    deep = wide // kt
    out_rows = block // kt
    selector = jnp.where(
        lax.broadcasted_iota(jnp.int32, (out_rows, deep), 1) // TIMES
        == lax.broadcasted_iota(jnp.int32, (out_rows, deep), 0),
        1.0,
        0.0,
    ).astype(bf16)
    first_gains = expand(start_gains)
    for j in range(half):
        for h in range(2):
            c = j + half * h
            loads[(0, c)].wait()
            loads[(1, c)].wait()
            v_re, v_im = vis[0, c].astype(f32), vis[1, c].astype(f32)
            m_re, m_im = sky[0, c].astype(f32), sky[1, c].astype(f32)
            for i, value in enumerate(
                (v_re * m_re + v_im * m_im, v_im * m_re - v_re * m_im, m_re * m_re + m_im * m_im)
            ):
                high = value.astype(bf16)
                prod[i, h * block : (h + 1) * block] = high
                prod[i, lanes + h * block : lanes + (h + 1) * block] = (value - high.astype(f32)).astype(bf16)
        for i, dst in enumerate((cross_re, cross_im, power)):
            for t in range(kt):
                total = lax.dot_general(
                    selector,
                    prod[i, :, t * deep : (t + 1) * deep],
                    (((1,), (1,)), ((), ())),
                    preferred_element_type=f32,
                )
                rows = slice(t * out_rows, (t + 1) * out_rows)
                dst[j, rows] = (total[:, :lanes] + total[:, lanes:]) * weight[rows]
        contract(0, first_gains, j)

    pl.semaphore_wait(barrier, n_col + n_sub + n_row - 3)

    def copy_of(src, dst, ssem, rsem, axis, peer):
        return pltpu.make_async_remote_copy(
            src_ref=src, dst_ref=dst, send_sem=ssem, recv_sem=rsem,
            device_id={axis: peer}, device_id_type=MESH,
        )

    def update(total, previous):
        den = total[channels:] + 1.0
        quotient = total[:channels] / jnp.concatenate([den, den], axis=0)
        return 0.5 * (quotient + previous)

    def mean_of(updated):
        re = jnp.sum(updated[:half], axis=0, keepdims=True)
        im = jnp.sum(updated[half:], axis=0, keepdims=True)
        packed = jnp.where(low, re, im)
        other = jnp.where(low, im, re)
        return (packed + pltpu.roll(other, block, 1)) / channels

    def over_sub(step, updated):
        mean = mean_of(updated)
        ysend[step] = mean
        copies = []
        for d in far_first(n_sub):
            copy = copy_of(
                ysend.at[step], ybuf.at[step, sub], y_ssem.at[step, d], y_rsem.at[step, sub],
                "sub", lax.rem(sub + d, n_sub),
            )
            copy.start()
            copies.append(copy)
        total = mean
        for d in range(1, n_sub):
            peer = lax.rem(sub + d, n_sub)
            copy_of(ysend.at[step], ybuf.at[step, peer], y_ssem.at[step, d], y_rsem.at[step, peer],
                    "sub", peer).wait_recv()
            total = total + ybuf[step, peer]
        delta = 0.5 * (total / n_sub - mean)
        turned = pltpu.roll(delta, block, 1)
        d_re = jnp.where(low, delta, turned)
        d_im = jnp.where(low, turned, delta)
        shift = jnp.concatenate(
            [jnp.broadcast_to(d_re, (half, lanes)), jnp.broadcast_to(d_im, (half, lanes))], axis=0
        )
        for copy in copies:
            copy.wait_send()
        return updated + shift

    for step in range(ITERS - 1):
        def to_hub(step=step):
            return copy_of(zsend.at[step], zbuf.at[step, col], z_ssem.at[step, 0], z_rsem.at[step, col],
                           "col", row)

        @pl.when(jnp.logical_not(hub))
        def _(step=step):
            to_hub().start()

        @pl.when(hub)
        def _(step=step):
            total = zsend[step]
            for d in range(1, n_col):
                peer = lax.rem(col + d, n_col)
                copy_of(zsend.at[step], zbuf.at[step, peer], z_ssem.at[step, 0], z_rsem.at[step, peer],
                        "col", peer).wait_recv()
                total = total + zbuf[step, peer]
            previous = start_gains if step == 0 else gsend[step - 1]
            gains = over_sub(step, update(total, previous))
            gsend[step] = gains
            copies = []
            for d in far_first(n_row):
                copy = copy_of(gsend.at[step], gbuf.at[step], g_ssem.at[step, d], g_rsem.at[step],
                               "row", lax.rem(row + d, n_row))
                copy.start()
                copies.append(copy)
            if step == ITERS - 2:
                for d in far_first(n_col):
                    copy = copy_of(gsend.at[step], pbuf, p_ssem.at[d], p_rsem, "col", lax.rem(col + d, n_col))
                    copy.start()
                    copies.append(copy)
                pbuf[...] = gains
            gbuf[step] = gains
            for copy in copies:
                copy.wait_send()

        @pl.when(jnp.logical_not(hub))
        def _(step=step):
            copy_of(gsend.at[step], gbuf.at[step], g_ssem.at[step, 0], g_rsem.at[step], "row", col).wait_recv()
            to_hub().wait_send()

        wide_gains = expand(gbuf[step])
        for j in range(half):
            contract(step + 1, wide_gains, j)

    step = ITERS - 1
    copies = []
    for d in far_first(n_col):
        copy = copy_of(zsend.at[step], zbuf.at[step, col], z_ssem.at[step, d], z_rsem.at[step, col],
                       "col", lax.rem(col + d, n_col))
        copy.start()
        copies.append(copy)

    @pl.when(jnp.logical_not(hub))
    def _():
        copy_of(gsend.at[0], pbuf, p_ssem.at[0], p_rsem, "col", row).wait_recv()

    total = zsend[step]
    for d in range(1, n_col):
        peer = lax.rem(col + d, n_col)
        copy_of(zsend.at[step], zbuf.at[step, peer], z_ssem.at[step, d], z_rsem.at[step, peer],
                "col", peer).wait_recv()
        total = total + zbuf[step, peer]
    gains = over_sub(step, update(total, pbuf[...]))
    fsend[...] = gains
    for d in far_first(n_row):
        copy = copy_of(fsend, fbuf.at[row], f_ssem.at[d], f_rsem.at[row], "row", lax.rem(row + d, n_row))
        copy.start()
        copies.append(copy)
    fbuf[row] = gains
    for d in range(1, n_row):
        peer = lax.rem(row + d, n_row)
        copy_of(fsend, fbuf.at[peer], f_ssem.at[d], f_rsem.at[peer], "row", peer).wait_recv()
    for m in range(n_row // 2):
        a, b = fbuf[2 * m], fbuf[2 * m + 1]
        first = jnp.where(low, a, pltpu.roll(b, block, 1))
        second = jnp.where(low, pltpu.roll(a, block, 1), b)
        at = slice(m * lanes, (m + 1) * lanes)
        for i in range(2):
            out_ref[i, :, at] = jnp.concatenate(
                [first[i * half : (i + 1) * half], second[i * half : (i + 1) * half]], axis=0
            )
    for copy in copies:
        copy.wait_send()


def body(visibility, sky_model, antenna_flags, gains_init):
    n_sub, n_row, n_col = (lax.axis_size(axis) for axis in ("sub", "row", "col"))
    _, channels, block, wide = visibility.shape
    lanes = 2 * block
    half = channels // 2
    f32, bf16 = jnp.float32, jnp.bfloat16
    dma = pltpu.SemaphoreType.DMA
    return pl.pallas_call(
        functools.partial(kernel, (n_sub, n_row, n_col, block, channels)),
        out_shape=jax.ShapeDtypeStruct(gains_init.shape, f32),
        in_specs=[
            pl.BlockSpec(memory_space=pl.ANY),
            pl.BlockSpec(memory_space=pl.ANY),
            pl.BlockSpec(memory_space=pltpu.VMEM),
            pl.BlockSpec(memory_space=pltpu.VMEM),
        ],
        out_specs=pl.BlockSpec(memory_space=pltpu.VMEM),
        scratch_shapes=[
            pltpu.VMEM(visibility.shape, bf16),
            pltpu.VMEM(visibility.shape, bf16),
            pltpu.VMEM((3, 2 * lanes, wide), bf16),
            pltpu.VMEM((half, block, lanes), f32),
            pltpu.VMEM((half, block, lanes), f32),
            pltpu.VMEM((half, block, lanes), f32),
            pltpu.VMEM((6 * channels, channels * lanes), bf16),
            pltpu.VMEM((ITERS, 3 * half, lanes), f32),
            pltpu.VMEM((ITERS, n_col, 3 * half, lanes), f32),
            pltpu.VMEM((ITERS, 1, lanes), f32),
            pltpu.VMEM((ITERS, n_sub, 1, lanes), f32),
            pltpu.VMEM((ITERS - 1, channels, lanes), f32),
            pltpu.VMEM((ITERS - 1, channels, lanes), f32),
            pltpu.VMEM((channels, lanes), f32),
            pltpu.VMEM((channels, lanes), f32),
            pltpu.VMEM((n_row, channels, lanes), f32),
            dma((2, channels)),
            dma((ITERS, n_col)),
            dma((ITERS, n_col)),
            dma((ITERS, n_sub)),
            dma((ITERS, n_sub)),
            dma((ITERS - 1, n_row)),
            dma((ITERS - 1,)),
            dma((n_col,)),
            dma,
            dma((n_row,)),
            dma((n_row,)),
        ],
        compiler_params=pltpu.CompilerParams(collective_id=0, has_side_effects=True),
        name="stefcal",
    )(visibility, sky_model, antenna_flags, gains_init)


def solution(mesh):
    return jax.shard_map(
        body,
        mesh=mesh,
        in_specs=(
            P(None, "sub", "row", "col"),
            P(None, "sub", "row", "col"),
            P("sub", None),
            P(None, "sub", None),
        ),
        out_specs=P(None, "sub", None),
        check_vma=False,
    )
```

time: 124 us -> 57.4 us (0.46)
  blocking collectives: 100 us -> 0 us
  Pallas kernels: 0 us -> 55.7 us
  matrix products: 11.9 us -> 0 us
  other arithmetic: 7.49 us -> 0 us
  local copies, waits for them, and re-layouts: 3.88 us -> 1.38 us
    all_to_all x9 -> x0, blocking collectives: 100 us -> none  [copy_for_each(): lax.all_to_all(jnp.broadcast_to(array[None], (devices, *array.shape)), ax...]
    pallas_call x0 -> x1, Pallas kernels: none -> 55.7 us  [body(): pl.pallas_call(functools.partial(kernel, (n_sub, n_row, n_col, block, cha...]
    dot_general x18 -> x0, matrix products: 11.9 us -> none  [the longest x15 7.86 us: contract(): jnp.einsum('cpq,cq->cp', matrix, vector, precision=lax.Precision.HIGHEST)]
    all_to_all x9 -> x0, other arithmetic: 6.41 us -> none  [copy_for_each(): lax.all_to_all(jnp.broadcast_to(array[None], (devices, *array.shape)), ax...]
where the time goes in v1:
time: 57.4 us; the launch traced here: 57.1 us
  Pallas kernels  55.7 us (97%)
  local copies, waits for them, and re-layouts  1.38 us (2%)
    pallas_call x1, Pallas kernels, body(): pl.pallas_call(functools.partial(kernel, (n_sub, n_row, n_col, block, cha...  55.7 us
    unnamed x1, local copies, waits for them, and re-layouts  1.38 us

profile of v1, /device:TPU:1, one launch (start us, length us, event | category | flops | bytes accessed | tf_op | source)
XLA Modules:
  0.0 57.1 jit_solution(15703989240253450333)
XLA Ops:
  0.0 55.7 %stefcal.1 = f32[2,8,512]{2,1,0:T(8,128)} custom-call(bf16[2,8,64,512]{3,2,1,0:T(8,128)(2,1)} %vis_ref.1, bf16[2,8,64,512]{3,2,1,0:T(8,128)(2,1)} %sky_ref.1, s32[1,512]{1,0:T(1,128)} %flag_ref.1, f32[2,8,512]{2,1,0:T(8,128)} %init_ref.1), custom_call_target="tpu_custom_call" | custom-call | tf_op jit(solution)/shard_map/stefcal/pallas_call | solution.py:280
  55.7 1.4 %copy.6 = f32[2,8,512]{2,1,0:T(8,128)} copy(f32[2,8,512]{2,1,0:T(8,128)} %stefcal.1) | data formatting | bytes 65536
